TPU v7x, 32 devices: a whole 2x2x4 slice. The times are simulated.
32 devices in a mesh: seq: 8 (over y, x, core), head: 4 (over z).
Axes of the slice: x: 2, y: 2, z: 4, core: 2. Of those that a mesh axis runs over, the one named last changes fastest.
Arguments:
- queries: bfloat16 [2048, 4096], P('seq', 'head'), may hold values from -7.1875 to 7.1875
- keys: bfloat16 [2048, 1024], P(('seq', 'head')), may hold values from -7.1875 to 7.1875
- values: bfloat16 [2048, 1024], P(('seq', 'head')), may hold values from -6 to 6
- outputs: bfloat16 [2048, 4096], P('seq', 'head'), may hold values from -1.1953125 to 1.1953125
- out_grad: bfloat16 [2048, 4096], P('seq', 'head'), may hold values from -6 to 6
- log_norm: float32 [32, 2048], P('head', 'seq'), as said below
- block_order: int32 [16], replicated, may hold values from 0 to 15, as said below
Outputs:
- query_grad: bfloat16 [2048, 4096], P('seq', 'head')
- key_gradient_rows: bfloat16 [2048, 1024], P(('seq', 'head'))
- value_gradient_rows: bfloat16 [2048, 1024], P(('seq', 'head'))
Inputs may be any that keep to these rules, and one draw needn't show every extreme that they name: `block_order`: A permutation of 0 to 15. log_norm[h, i] lies within 0.6 of one plus the natural logarithm of 1 + pos[i].
All inputs are finite; a program needn't handle non-finite values.
Results may differ from a plain program's by a relative error of at most 0.014.
Values may be sent and summed in bfloat16 or wider, within the bound.
A program may use at most 192 MiB of HBM per device.

v0:
```python
import jax
import jax.numpy as jnp
from jax import lax
from jax.sharding import PartitionSpec as P

QUERY_HEADS = 32
KEY_VALUE_HEADS = 8
HEAD_SIZE = 128


def row_positions(block_order, first_row, count, half):
    rows_here = first_row + jnp.arange(count, dtype=jnp.int32)
    blocks = rows_here // half
    table = jnp.arange(block_order.shape[0], dtype=jnp.int32)
    picked = jnp.sum(jnp.where(blocks[:, None] == table[None, :], block_order[None, :], 0), 1)
    return picked * half + rows_here % half


def masked_terms(q_blk, dout_blk, lse_blk, delta_blk, q_pos, k_blk, v_blk, k_pos):
    scale = HEAD_SIZE ** (-0.5)
    scores = jnp.einsum("tgrd,ngd->grtn", q_blk, k_blk, preferred_element_type=jnp.float32) * scale
    visible = k_pos[None, :] <= q_pos[:, None]
    prob = jnp.where(visible, jnp.exp(scores - lse_blk[..., None]), 0.0)
    dprob = jnp.einsum("tgrd,ngd->grtn", dout_blk, v_blk, preferred_element_type=jnp.float32)
    dscore = prob * (dprob - delta_blk[..., None])
    prob_low = prob.astype(jnp.bfloat16)
    dscore_low = dscore.astype(jnp.bfloat16)
    queries_gradient = (
        jnp.einsum("grtn,ngd->tgrd", dscore_low, k_blk, preferred_element_type=jnp.float32) * scale
    )
    keys_gradient = (
        jnp.einsum("grtn,tgrd->ngd", dscore_low, q_blk, preferred_element_type=jnp.float32) * scale
    )
    values_gradient = jnp.einsum(
        "grtn,tgrd->ngd", prob_low, dout_blk, preferred_element_type=jnp.float32
    )
    return (queries_gradient, keys_gradient, values_gradient)


def step_rows(count):
    step = count
    while step > 1024 and step % 2 == 0:
        step = step // 2
    return step


def local(queries, keys, values, outputs, out_grad, log_norm, block_order):
    index = lax.axis_index("seq")
    rows = queries.shape[0]
    half = rows // 2
    group_ratio = QUERY_HEADS // KEY_VALUE_HEADS
    k_loc, v_loc = (
        lax.all_to_all(keys, "head", split_axis=1, concat_axis=0, tiled=True),
        lax.all_to_all(values, "head", split_axis=1, concat_axis=0, tiled=True),
    )
    q_cols = queries.shape[1]
    heads_here = q_cols // HEAD_SIZE
    groups = heads_here // group_ratio
    k_cols = k_loc.shape[1]
    delta = jnp.sum(
        (out_grad.astype(jnp.float32) * outputs.astype(jnp.float32)).reshape(
            rows, heads_here, HEAD_SIZE
        ),
        -1,
    )
    own_pair = lax.dynamic_slice(block_order, (2 * index,), (2,))
    own_blocks = (own_pair[0], own_pair[1])
    offset = jnp.arange(half, dtype=jnp.int32)
    own_pos = jnp.concatenate([own_blocks[0] * half + offset, own_blocks[1] * half + offset], 0)
    k_own = k_loc.reshape(rows, groups, HEAD_SIZE)
    v_own = v_loc.reshape(rows, groups, HEAD_SIZE)
    keys_gradient = None
    values_gradient = None
    all_lse, all_delta = (
        lax.all_gather(log_norm.T, "seq", axis=0, tiled=True),
        lax.all_gather(delta, "seq", axis=0, tiled=True),
    )
    k_zero = jnp.zeros((rows, groups, HEAD_SIZE), jnp.float32)
    grad_k = k_zero
    grad_v = k_zero
    q_piece = lax.all_gather(queries, "seq", axis=0, tiled=True)
    dout_piece = lax.all_gather(out_grad, "seq", axis=0, tiled=True)
    count = q_piece.shape[0]
    step = step_rows(count)

    def one(acc, i):
        q_blk = lax.dynamic_slice_in_dim(q_piece, i * step, step, 0).reshape(
            step, groups, group_ratio, HEAD_SIZE
        )
        dout_blk = lax.dynamic_slice_in_dim(dout_piece, i * step, step, 0).reshape(
            step, groups, group_ratio, HEAD_SIZE
        )
        row0 = i * step
        lse_blk = lax.dynamic_slice_in_dim(all_lse, row0, step, 0).T.reshape(
            groups, group_ratio, step
        )
        delta_blk = lax.dynamic_slice_in_dim(all_delta, row0, step, 0).T.reshape(
            groups, group_ratio, step
        )
        q_pos = row_positions(block_order, row0, step, half)
        terms = masked_terms(q_blk, dout_blk, lse_blk, delta_blk, q_pos, k_own, v_own, own_pos)
        return ((acc[0] + terms[1], acc[1] + terms[2]), terms[0].reshape(step, q_cols))

    (grad_k, grad_v), stacked = lax.scan(
        one, (grad_k, grad_v), jnp.arange(count // step, dtype=jnp.int32)
    )
    grad_q_all = stacked.reshape(count, q_cols)
    grad_k, grad_v, grad_q_all = (grad_k, grad_v, grad_q_all)
    queries_gradient = lax.psum_scatter(
        grad_q_all.astype(jnp.bfloat16), "seq", scatter_dimension=0, tiled=True
    )
    keys_gradient = grad_k.reshape(rows, k_cols)
    values_gradient = grad_v.reshape(rows, k_cols)
    low_k = keys_gradient.astype(jnp.bfloat16)
    low_v = values_gradient.astype(jnp.bfloat16)
    key_gradient_rows, value_gradient_rows = (
        lax.all_to_all(low_k, "head", split_axis=0, concat_axis=1, tiled=True),
        lax.all_to_all(low_v, "head", split_axis=0, concat_axis=1, tiled=True),
    )
    return (queries_gradient, key_gradient_rows, value_gradient_rows)


def solution(mesh):
    in_specs = (
        P("seq", "head"),
        P(("seq", "head"), None),
        P(("seq", "head"), None),
        P("seq", "head"),
        P("seq", "head"),
        P("head", "seq"),
        P(),
    )
    out_specs = (P("seq", "head"), P(("seq", "head"), None), P(("seq", "head"), None))
    return jax.shard_map(local, mesh=mesh, in_specs=in_specs, out_specs=out_specs, check_vma=False)
```

profile of v0, /device:TPU:0, one launch (start us, length us, event | category | flops | bytes accessed | tf_op | source)
XLA Modules:
  0.0 188.3 jit_solution(1644582682500245099)
XLA Ops:
  7.2 2.1 %copy.61 = bf16[256,1024]{0,1:T(8,128)(2,1)} copy(bf16[256,1024]{1,0:T(8,128)(2,1)} %param.9) | data formatting | bytes 1048576 | tf_op args[0]
  9.4 2.1 %copy.63 = bf16[256,1024]{0,1:T(8,128)(2,1)} copy(bf16[256,1024]{1,0:T(8,128)(2,1)} %param.13) | data formatting | bytes 1048576 | tf_op args[4]
  11.6 1.6 copy.90
  13.1 6.3 %all-to-all-start = ((bf16[64,4,256]{2,0,1:T(8,128)(2,1)}), bf16[64,4,256]{2,0,1:T(8,128)(2,1)S(1)}, u32[]{:S(2)}, u32[]{:S(2)}) async-start(bf16[64,4,256]{2,0,1:T(8,128)(2,1)} %bitcast.94), calls=%async_computation | async-start | bytes 262144 | tf_op jit(solution)/shard_map/all_to_all | solution.py:53
  19.5 0.7 dynamic_slice.34
  20.2 0.6 fusion.29
  22.1 1.6 copy.89
  23.8 0.2 copy.86
  24.0 0.3 reduce_sum.21
  24.4 12.3 %all_gather.15 = f32[2048,8]{1,0:T(8,128)S(1)} all-gather(f32[256,8]{1,0:T(8,128)S(1)} %reduce_sum.21), channel_id=1, replica_groups=mesh['seq'=8,'head'=4] {'seq'}, dimensions={0}, use_global_device_ids=true | all-gather | bytes 73728 | tf_op jit(solution)/shard_map/all_gather | solution.py:76
  36.6 0.3 copy.67
  36.9 8.4 %all_gather.13 = f32[2048,8]{0,1:T(8,128)S(1)} all-gather(f32[256,8]{0,1:T(8,128)S(1)} %bitcast.150), channel_id=1, replica_groups=mesh['seq'=8,'head'=4] {'seq'}, dimensions={0}, use_global_device_ids=true | all-gather | bytes 73728 | tf_op jit(solution)/shard_map/all_gather | solution.py:75
  45.3 5.0 %all-to-all-start.1 = ((bf16[64,4,256]{2,0,1:T(8,128)(2,1)}), bf16[64,4,256]{2,0,1:T(8,128)(2,1)S(1)}, u32[]{:S(2)}, u32[]{:S(2)}) async-start(bf16[64,4,256]{2,0,1:T(8,128)(2,1)} %bitcast.93), calls=%async_computation.1 | async-start | bytes 262144 | tf_op jit(solution)/shard_map/all_to_all | solution.py:54
  50.5 6.2 %all-to-all-done.1 = bf16[64,4,256]{2,0,1:T(8,128)(2,1)S(1)} async-done(((bf16[64,4,256]{2,0,1:T(8,128)(2,1)}), bf16[64,4,256]{2,0,1:T(8,128)(2,1)S(1)}, u32[]{:S(2)}, u32[]{:S(2)}) %all-to-all-start.1) | async-done | bytes 131104 | tf_op jit(solution)/shard_map/all_to_all | solution.py:54
  56.8 33.3 %all-gather.5.cloned.1.call-done = bf16[2048,1024]{0,1:T(8,128)(2,1)} async-done(((bf16[256,1024]{0,1:T(8,128)(2,1)}), bf16[2048,1024]{0,1:T(8,128)(2,1)}) %all-gather.5.cloned.1.call-update) | async-done | bytes 4194320 | tf_op jit(solution)/shard_map/all_gather | solution.py:82
  90.2 34.1 %while.17 = (s32[]{:T(128)}, f32[256,2,128]{0,2,1:T(8,128)S(1)}, f32[256,2,128]{0,2,1:T(8,128)S(1)}, bf16[2,1024,1024]{1,2,0:T(8,128)(2,1)}, s32[2]{0:T(128)S(1)...) while((s32[]{:T(128)}, f32[256,2,128]{0,2,1:T(8,128)S(1)}, ...), condition=%wide.region_3.4_spmd.clone, body=%wide.region_1.3_spmd.clone.sunk | while | flops 2708091904 | bytes 96986472 | solution.py:104
  90.2 0.6 dynamic_slice.49
  91.6 0.2 broadcast_compare_fusion.2
  91.8 2.7 %constant_dynamic-slice_fusion.3 = (bf16[1024,1024]{0,1:T(8,128)(2,1)S(1)}, bf16[1024,1024]{0,1:T(8,128)(2,1)S(1)}) fusion(bf16[2048,1024]{0,1:T(8,128)(2,1)} %get-tuple-element.431, s32[]{:T(128)S(6)} %select_n.86, bf16[2048,1024]{0,1:T(8,128)(2,1)} %get-tuple-element.426), kind=kLoop, calls=%fused_computation.39.clone.1 | loop fusion | bytes 8388612 | tf_op jit(solution)/shard_map/while/body/eval_jaxpr/dynamic_slice | solution.py:90
  94.5 1.3 fusion.61
  95.8 2.0 %fusion.65 = f32[256,2,128]{0,2,1:T(8,128)S(1)} fusion(bf16[1024,2,4,128]{0,3,2,1:T(8,128)(2,1)S(1)} %bitcast.138, f32[2,1024,4,256]{3,1,2,0:T(8,128)S(1)} %fusion.61, f32[2,4,1024]{2,1,0:T(4,128)S(1)} %sub.96, pred[1024,256]{1,0:T(8,128)(4,1)S(1)} %broadcast_compare_fusion.2, f32[256,2,128]{0,2,1:T(8,128)S(1)} %get-tuple-element.406, pred[]{:T(512)S(6)} %compare.15), kind=kOutput, calls=%fused_computation.15.clone.1 | convolution fusion | flops 545390592 | bytes 11304961 | tf_op jit(solution)/shard_map/while/body/eval_jaxpr/grtn,tgrd->ngd/dot_general | solution.py:34
  97.8 4.2 %fusion.63 = bf16[2,4,1024,256]{3,2,1,0:T(8,128)(2,1)S(1)} fusion(f32[2,1024,4,256]{3,1,2,0:T(8,128)S(1)} %fusion.61, f32[2,4,1024]{2,1,0:T(4,128)S(1)} %sub.95, f32[2,4,1024]{2,1,0:T(4,128)S(1)} %sub.96, pred[1024,256]{1,0:T(8,128)(4,1)S(1)} %broadcast_compare_fusion.2, bf16[1024,2,4,128]{0,3,2,1:T(8,128)(2,1)S(1)} %bitcast.139, ...), kind=kOutput, calls=%fused_computation.2.clone.1 | convolution fusion | flops 549453824 | bytes 15138816 | tf_op jit(solution)/shard_map/while/body/eval_jaxpr/tgrd,ngd->grtn/dot_general | solution.py:24
  102.0 0.7 fusion.64
  102.8 1.5 convolution_multiply_fusion.2
  104.3 0.7 copy-done
  105.0 0.3 constant_dynamic-update-slice_fusion.2
  105.3 2.0 %copy-done.1 = bf16[2,1024,1024]{1,2,0:T(8,128)(2,1)} copy-done((bf16[2,1024,1024]{1,2,0:T(8,128)(2,1)}, bf16[2,1024,1024]{1,2,0:T(8,128)(2,1)S(1)}, u32[]{:S(2)}) %copy-start.1) | copy-done | bytes 4194328 | tf_op jit(solution)/shard_map/while
  107.2 0.6 dynamic_slice.49
  108.7 0.2 broadcast_compare_fusion.2
  108.9 2.7 %constant_dynamic-slice_fusion.3 = (bf16[1024,1024]{0,1:T(8,128)(2,1)S(1)}, bf16[1024,1024]{0,1:T(8,128)(2,1)S(1)}) fusion(bf16[2048,1024]{0,1:T(8,128)(2,1)} %get-tuple-element.431, s32[]{:T(128)S(6)} %select_n.86, bf16[2048,1024]{0,1:T(8,128)(2,1)} %get-tuple-element.426), kind=kLoop, calls=%fused_computation.39.clone.1 | loop fusion | bytes 8388612 | tf_op jit(solution)/shard_map/while/body/eval_jaxpr/dynamic_slice | solution.py:90
  111.5 1.3 fusion.61
  112.8 2.0 %fusion.65 = f32[256,2,128]{0,2,1:T(8,128)S(1)} fusion(bf16[1024,2,4,128]{0,3,2,1:T(8,128)(2,1)S(1)} %bitcast.138, f32[2,1024,4,256]{3,1,2,0:T(8,128)S(1)} %fusion.61, f32[2,4,1024]{2,1,0:T(4,128)S(1)} %sub.96, pred[1024,256]{1,0:T(8,128)(4,1)S(1)} %broadcast_compare_fusion.2, f32[256,2,128]{0,2,1:T(8,128)S(1)} %get-tuple-element.406, pred[]{:T(512)S(6)} %compare.15), kind=kOutput, calls=%fused_computation.15.clone.1 | convolution fusion | flops 545390592 | bytes 11304961 | tf_op jit(solution)/shard_map/while/body/eval_jaxpr/grtn,tgrd->ngd/dot_general | solution.py:34
  114.8 4.2 %fusion.63 = bf16[2,4,1024,256]{3,2,1,0:T(8,128)(2,1)S(1)} fusion(f32[2,1024,4,256]{3,1,2,0:T(8,128)S(1)} %fusion.61, f32[2,4,1024]{2,1,0:T(4,128)S(1)} %sub.95, f32[2,4,1024]{2,1,0:T(4,128)S(1)} %sub.96, pred[1024,256]{1,0:T(8,128)(4,1)S(1)} %broadcast_compare_fusion.2, bf16[1024,2,4,128]{0,3,2,1:T(8,128)(2,1)S(1)} %bitcast.139, ...), kind=kOutput, calls=%fused_computation.2.clone.1 | convolution fusion | flops 549453824 | bytes 15138816 | tf_op jit(solution)/shard_map/while/body/eval_jaxpr/tgrd,ngd->grtn/dot_general | solution.py:24
  119.1 0.7 fusion.64
  119.8 1.5 convolution_multiply_fusion.2
  121.3 0.7 copy-done
  122.0 0.3 constant_dynamic-update-slice_fusion.2
  122.3 2.0 %copy-done.1 = bf16[2,1024,1024]{1,2,0:T(8,128)(2,1)} copy-done((bf16[2,1024,1024]{1,2,0:T(8,128)(2,1)}, bf16[2,1024,1024]{1,2,0:T(8,128)(2,1)S(1)}, u32[]{:S(2)}) %copy-start.1) | copy-done | bytes 4194328 | tf_op jit(solution)/shard_map/while
  124.3 6.2 %copy.68 = bf16[2,1024,1024]{2,1,0:T(8,128)(2,1)} copy(bf16[2,1024,1024]{1,2,0:T(8,128)(2,1)} %get-tuple-element.169) | data formatting | bytes 8388608 | tf_op jit(solution)/shard_map/convert_element_type | solution.py:110
  130.6 0.7 convert_element_type.43
  131.4 4.6 %all-to-all-start.2 = ((bf16[4,64,256]{2,1,0:T(8,128)(2,1)}), bf16[4,64,256]{2,1,0:T(8,128)(2,1)S(1)}, u32[]{:S(2)}, u32[]{:S(2)}) async-start(bf16[4,64,256]{2,1,0:T(8,128)(2,1)} %convert_element_type.43), calls=%async_computation.3 | async-start | bytes 262144 | tf_op jit(solution)/shard_map/all_to_all | solution.py:117
  136.1 0.7 convert_element_type.45
  136.9 5.4 %all-to-all-done.2 = bf16[4,64,256]{2,1,0:T(8,128)(2,1)S(1)} async-done(((bf16[4,64,256]{2,1,0:T(8,128)(2,1)}), bf16[4,64,256]{2,1,0:T(8,128)(2,1)S(1)}, u32[]{:S(2)}, u32[]{:S(2)}) %all-to-all-start.2) | async-done | bytes 131104 | tf_op jit(solution)/shard_map/all_to_all | solution.py:117
  142.3 3.3 %all-to-all-start.3 = ((bf16[4,64,256]{2,1,0:T(8,128)(2,1)}), bf16[4,64,256]{2,1,0:T(8,128)(2,1)S(1)}, u32[]{:S(2)}, u32[]{:S(2)}) async-start(bf16[4,64,256]{2,1,0:T(8,128)(2,1)} %convert_element_type.45), calls=%async_computation.4 | async-start | bytes 262144 | tf_op jit(solution)/shard_map/all_to_all | solution.py:118
  145.6 0.7 copy.84
  146.3 5.2 %all-to-all-done.3 = bf16[4,64,256]{2,1,0:T(8,128)(2,1)S(1)} async-done(((bf16[4,64,256]{2,1,0:T(8,128)(2,1)}), bf16[4,64,256]{2,1,0:T(8,128)(2,1)S(1)}, u32[]{:S(2)}, u32[]{:S(2)}) %all-to-all-start.3) | async-done | bytes 131104 | tf_op jit(solution)/shard_map/all_to_all | solution.py:118
  151.5 0.7 copy.85
  152.2 29.6 %reduce-scatter.2.cloned.1.call-done = bf16[256,1024]{1,0:T(8,128)(2,1)} async-done(((bf16[2048,1024]{1,0:T(8,128)(2,1)}), bf16[256,1024]{1,0:T(8,128)(2,1)}) %reduce-scatter.2.cloned.1.call-update) | async-done | bytes 524304 | tf_op jit(solution)/shard_map/reduce_scatter | solution.py:109
  (47 shorter events, 1.1 us)
Async XLA Ops:
  7.2 16.5 %copy-start.2 = (bf16[256,1024]{1,0:T(8,128)(2,1)S(1)}, bf16[256,1024]{1,0:T(8,128)(2,1)}, u32[]{:S(2)}) copy-start(bf16[256,1024]{1,0:T(8,128)(2,1)} %param.13) | copy-start | bytes 1572868
  7.2 16.5 %copy-start.3 = (bf16[256,1024]{1,0:T(8,128)(2,1)S(1)}, bf16[256,1024]{1,0:T(8,128)(2,1)}, u32[]{:S(2)}) copy-start(bf16[256,1024]{1,0:T(8,128)(2,1)} %param.12) | copy-start | bytes 1572868
  7.2 49.7 %all-gather.3.cloned.1.call-start = ((), (), s32[]{:S(2)}) async-start(), calls=%async_computation.5 | async-start | bytes 4718592 | tf_op jit(solution)/shard_map/all_gather | solution.py:81
  9.4 80.8 %all-gather.5.cloned.1.call-start = ((), (), s32[]{:S(2)}) async-start(), calls=%async_computation.6 | async-start | bytes 4718592 | tf_op jit(solution)/shard_map/all_gather | solution.py:82
  11.5 25.4 %copy-start.5 = (f32[8,256]{1,0:T(8,128)S(1)}, f32[8,256]{1,0:T(8,128)}, u32[]{:S(2)}) copy-start(f32[8,256]{1,0:T(8,128)} %param.14) | copy-start | bytes 24580
  13.1 32.2 %all-to-all-start = ((bf16[64,4,256]{2,0,1:T(8,128)(2,1)}), bf16[64,4,256]{2,0,1:T(8,128)(2,1)S(1)}, u32[]{:S(2)}, u32[]{:S(2)}) async-start(bf16[64,4,256]{2,0,1:T(8,128)(2,1)} %bitcast.94), calls=%async_computation | async-start | bytes 262144 | tf_op jit(solution)/shard_map/all_to_all | solution.py:53
  23.7 66.5 %copy-start.4 = (s32[16]{0:T(128)S(1)}, s32[16]{0:T(128)}, u32[]{:S(2)}) copy-start(s32[16]{0:T(128)} %param.15) | copy-start | bytes 196
  45.3 11.4 %all-to-all-start.1 = ((bf16[64,4,256]{2,0,1:T(8,128)(2,1)}), bf16[64,4,256]{2,0,1:T(8,128)(2,1)S(1)}, u32[]{:S(2)}, u32[]{:S(2)}) async-start(bf16[64,4,256]{2,0,1:T(8,128)(2,1)} %bitcast.93), calls=%async_computation.1 | async-start | bytes 262144 | tf_op jit(solution)/shard_map/all_to_all | solution.py:54
  50.3 131.5 %reduce-scatter.2.cloned.1.call-start = ((), (), s32[]{:S(2)}) async-start(), calls=%async_computation.7 | async-start | bytes 4718592 | tf_op jit(solution)/shard_map/reduce_scatter | solution.py:109
  102.8 2.2 %copy-start = (bf16[2,1024,1024]{1,2,0:T(8,128)(2,1)S(1)}, bf16[2,1024,1024]{1,2,0:T(8,128)(2,1)}, u32[]{:S(2)}) copy-start(bf16[2,1024,1024]{1,2,0:T(8,128)(2,1)} %get-tuple-element.407) | copy-start | bytes 12582916 | tf_op jit(solution)/shard_map/while
  105.3 2.0 %copy-start.1 = (bf16[2,1024,1024]{1,2,0:T(8,128)(2,1)}, bf16[2,1024,1024]{1,2,0:T(8,128)(2,1)S(1)}, u32[]{:S(2)}) copy-start(bf16[2,1024,1024]{1,2,0:T(8,128)(2,1)S(1)} %constant_dynamic-update-slice_fusion.2) | copy-start | bytes 12582916 | tf_op jit(solution)/shard_map/while
  119.8 2.2 %copy-start = (bf16[2,1024,1024]{1,2,0:T(8,128)(2,1)S(1)}, bf16[2,1024,1024]{1,2,0:T(8,128)(2,1)}, u32[]{:S(2)}) copy-start(bf16[2,1024,1024]{1,2,0:T(8,128)(2,1)} %get-tuple-element.407) | copy-start | bytes 12582916 | tf_op jit(solution)/shard_map/while
  122.3 2.0 %copy-start.1 = (bf16[2,1024,1024]{1,2,0:T(8,128)(2,1)}, bf16[2,1024,1024]{1,2,0:T(8,128)(2,1)S(1)}, u32[]{:S(2)}) copy-start(bf16[2,1024,1024]{1,2,0:T(8,128)(2,1)S(1)} %constant_dynamic-update-slice_fusion.2) | copy-start | bytes 12582916 | tf_op jit(solution)/shard_map/while
  131.4 10.9 %all-to-all-start.2 = ((bf16[4,64,256]{2,1,0:T(8,128)(2,1)}), bf16[4,64,256]{2,1,0:T(8,128)(2,1)S(1)}, u32[]{:S(2)}, u32[]{:S(2)}) async-start(bf16[4,64,256]{2,1,0:T(8,128)(2,1)} %convert_element_type.43), calls=%async_computation.3 | async-start | bytes 262144 | tf_op jit(solution)/shard_map/all_to_all | solution.py:117
  142.3 9.2 %all-to-all-start.3 = ((bf16[4,64,256]{2,1,0:T(8,128)(2,1)}), bf16[4,64,256]{2,1,0:T(8,128)(2,1)S(1)}, u32[]{:S(2)}, u32[]{:S(2)}) async-start(bf16[4,64,256]{2,1,0:T(8,128)(2,1)} %convert_element_type.45), calls=%async_computation.4 | async-start | bytes 262144 | tf_op jit(solution)/shard_map/all_to_all | solution.py:118
Sparse Core Ops, SparseCore 0:
  10.4 40.4 all-gather.2
  52.8 37.3 all-gather.4
  130.6 51.1 reduce-scatter.1
where the time goes:
time: 189 us; the launch traced here: 188 us
  waiting for transfers between devices  79.9 us (42%)
  local copies, waits for them, and re-layouts  31.1 us (16%)
  blocking collectives  20.6 us (11%)
  matrix products  19.5 us (10%)
  starting transfers between devices  19.4 us (10%)
  between operations  15.1 us (8%)
    all_gather x1, waiting for transfers between devices, local(): dout_piece = lax.all_gather(out_grad, 'seq', axis=0, tiled=True)  33.3 us
    reduce_scatter x1, waiting for transfers between devices, local(): lax.psum_scatter(grad_q_all.astype(jnp.bfloat16), 'seq', scatter_dimensio...  29.6 us
    all_gather x1, blocking collectives, local(): lax.all_gather(delta, 'seq', axis=0, tiled=True)  12.3 us
    dot_general x2, matrix products, masked_terms(): jnp.einsum('tgrd,ngd->grtn', dout_blk, v_blk, preferred_element_type=jnp....  8.49 us
    all_gather x1, blocking collectives, local(): lax.all_gather(log_norm.T, 'seq', axis=0, tiled=True)  8.37 us
    all_to_all x1, starting transfers between devices, local(): lax.all_to_all(keys, 'head', split_axis=1, concat_axis=0, tiled=True)  6.35 us
    all_to_all x1, waiting for transfers between devices, local(): lax.all_to_all(values, 'head', split_axis=1, concat_axis=0, tiled=True)  6.25 us
    convert_element_type x1, local copies, waits for them, and re-layouts, local(): grad_q_all.astype(jnp.bfloat16)  6.2 us
  transfers between devices with their start and end apart: 7, of which 5 were waited for; matrix products, arithmetic and copies ran while one was open for 6% of the time, Pallas kernels for 0%

commit v1 on v0

v1 whole, which is shorter than its diff:
```python
import functools
import math

import jax
import jax.numpy as jnp
from jax import lax
from jax.experimental import pallas as pl
from jax.experimental.pallas import tpu as pltpu
from jax.sharding import PartitionSpec as P

QUERY_HEADS = 32
KEY_VALUE_HEADS = 8
HEAD_SIZE = 128
MESH = pl.DeviceIdType.MESH
NT = (((1,), (1,)), ((), ()))
F32 = jnp.float32
BF16 = jnp.bfloat16


def kernel(
    n_seq,
    n_head,
    q_in,
    k_in,
    v_in,
    o_in,
    do_in,
    lse_in,
    order,
    dq_out,
    dk_out,
    dv_out,
    qs,
    dos,
    o_all,
    do_all,
    lse,
    delta,
    kv,
    acc,
    dqt,
    dq_send,
    dq_recv,
    part_send,
    part_recv,
    last_send,
    last_recv,
    load_sem,
    first_send_sem,
    first_recv_sem,
    pair_send_sem,
    pair_recv_sem,
    kv_send_sem,
    kv_recv_sem,
    part_send_sem,
    part_recv_sem,
    last_send_sem,
    last_recv_sem,
    dq_sem,
):
    D = HEAD_SIZE
    R = QUERY_HEADS // KEY_VALUE_HEADS
    chips = n_seq // 2
    bits = (chips - 1).bit_length()
    steps = 2 * chips
    rows = q_in.shape[0]
    half = rows // 2
    piece = k_in.shape[0]
    me_s = lax.axis_index("seq")
    head = lax.axis_index("head")
    core = me_s % 2
    chip = me_s // 2
    mate = (core + 1) % 2
    mate_id = (chip * 2 + mate, head)
    scale = D ** (-0.5)

    def flip(a, d):
        return sum(((a // 2**i) % 2 + (d // 2**i) % 2) % 2 * 2**i for i in range(bits))

    def peer(d):
        return (flip(chip, d) * 2 + core, head)

    near = [(a, b) for b in range(n_head) for a in range(2) if (a, b) != (0, 0)]

    def near_at(a, b):
        return (core + a) % 2, (head + b) % n_head

    def lanes(start, size):
        return pl.ds(pl.multiple_of(start, D), size)

    loads = [
        pltpu.make_async_copy(o_in, o_all, load_sem.at[0]),
        pltpu.make_async_copy(do_in, do_all, load_sem.at[1]),
        pltpu.make_async_copy(lse_in, lse.at[0], load_sem.at[2]),
    ]
    mine = lanes((2 * head + core) * D, D)
    own_rows = pl.ds(pl.multiple_of(head * piece, piece), piece)
    loads.append(pltpu.make_async_copy(k_in.at[:, mine], kv.at[0, 0, 0, own_rows, :], load_sem.at[3]))
    loads.append(pltpu.make_async_copy(v_in.at[:, mine], kv.at[0, 0, 1, own_rows, :], load_sem.at[4]))
    for r in range(R):
        cols = lanes((core * R + r) * D, D)
        loads.append(pltpu.make_async_copy(q_in.at[:, cols], qs.at[0, r], load_sem.at[5 + r]))
        loads.append(pltpu.make_async_copy(do_in.at[:, cols], dos.at[0, r], load_sem.at[5 + R + r]))
    for copy in loads:
        copy.start()

    barrier = pltpu.get_barrier_semaphore()
    for a, b in near:
        c2, h2 = near_at(a, b)
        pl.semaphore_signal(barrier, inc=1, device_id=(chip * 2 + c2, h2), device_id_type=MESH)
    for d in range(1, chips):
        pl.semaphore_signal(barrier, inc=1, device_id=peer(d), device_id_type=MESH)
    pl.semaphore_wait(barrier, len(near) + chips - 1)

    first = {}
    for a, b in near:
        c2, h2 = near_at(a, b)
        for j, src in enumerate((k_in, v_in)):
            first[a, b, j] = pltpu.make_async_remote_copy(
                src_ref=src.at[:, lanes((2 * h2 + c2) * D, D)],
                dst_ref=kv.at[0, a, j, own_rows, :],
                send_sem=first_send_sem.at[a * n_head + b, j],
                recv_sem=first_recv_sem.at[a * n_head + b, j],
                device_id=(chip * 2 + c2, h2),
                device_id_type=MESH,
            )
    for key in sorted(first):
        first[key].start()
    pair = []

    def to_mate(src, dst, i):
        return pltpu.make_async_remote_copy(
            src_ref=src,
            dst_ref=dst,
            send_sem=pair_send_sem.at[i],
            recv_sem=pair_recv_sem.at[i],
            device_id=mate_id,
            device_id_type=MESH,
        )

    for r in range(R):
        cols = lanes((mate * R + r) * D, D)
        pair.append(to_mate(q_in.at[:, cols], qs.at[1, r], r))
        pair.append(to_mate(do_in.at[:, cols], dos.at[1, r], R + r))
    pair.append(to_mate(lse_in, lse.at[1], 2 * R))
    for copy in pair:
        copy.start()

    for copy in loads:
        copy.wait()
    for i in range(2 * R):
        prod = o_all[:, i * D : (i + 1) * D].astype(F32) * do_all[:, i * D : (i + 1) * D].astype(F32)
        delta[0, pl.ds(i, 1), :] = jnp.sum(prod.T, axis=0, keepdims=True)
    dqt[...] = jnp.zeros_like(dqt)
    acc[...] = jnp.zeros_like(acc)

    def kv_copy(d, hf):
        return pltpu.make_async_remote_copy(
            src_ref=kv.at[0, hf],
            dst_ref=kv.at[d, hf],
            send_sem=kv_send_sem.at[d, hf],
            recv_sem=kv_recv_sem.at[d, hf],
            device_id=peer(d),
            device_id_type=MESH,
        )

    for hf in range(2):
        for a, b, j in sorted(first):
            if a == hf:
                first[a, b, j].wait_recv()
        for d in range(1, min(chips, 3)):
            kv_copy(d, hf).start()
    for d in range(3, chips):
        for hf in range(2):
            kv_copy(d, hf).start()

    send_delta = to_mate(delta.at[0], delta.at[1], 2 * R + 1)
    send_delta.start()
    pair.append(send_delta)
    for copy in pair:
        copy.wait_recv()

    def part_copy(d, hf):
        return pltpu.make_async_remote_copy(
            src_ref=part_send.at[d, hf],
            dst_ref=part_recv.at[d, hf],
            send_sem=part_send_sem.at[d, hf],
            recv_sem=part_recv_sem.at[d, hf],
            device_id=peer(d),
            device_id_type=MESH,
        )

    dq_copy = pltpu.make_async_remote_copy(
        src_ref=dq_send.at[1],
        dst_ref=dq_recv,
        send_sem=dq_sem.at[0],
        recv_sem=dq_sem.at[1],
        device_id=mate_id,
        device_id_type=MESH,
    )

    def spots(index, shape, dim):
        off = lax.broadcasted_iota(jnp.int32, shape, dim)
        b0 = order[2 * index]
        b1 = order[2 * index + 1]
        return off + jnp.where(off < half, b0 * half, b1 * half - half)

    def step(t, carry):
        d = ((t + 1) // 2) % chips
        hf = (t + 1) % 2

        @pl.when(d > 0)
        def _():
            kv_copy(d, hf).wait_recv()

        def inner(i, carry):
            rr = (i + t // (steps - 1)) % 2
            kk = kv[d, hf, 0]
            vv = kv[d, hf, 1]
            kt = kk.T
            k_at = spots(flip(chip, d) * 2 + (core + hf) % 2, (rows, 1), 0)
            q_at = spots(chip * 2 + (core + rr) % 2, (1, rows), 1)
            mask = k_at <= q_at
            dk = None
            dv = None
            for r in range(R):
                qr = qs[rr, r]
                dor = dos[rr, r]
                s = lax.dot_general(kk, qr, NT, preferred_element_type=F32)
                dp = lax.dot_general(vv, dor, NT, preferred_element_type=F32)
                row = pl.ds(core * R + r, 1)
                l2 = lse[rr, row, :] * math.log2(math.e)
                dl = delta[rr, row, :]
                prob = jnp.where(mask, jnp.exp2(s * (scale * math.log2(math.e)) - l2), 0.0)
                ds = (prob * (dp - dl)).astype(BF16)
                tv = jnp.dot(prob.astype(BF16), dor, preferred_element_type=F32)
                tk = jnp.dot(ds, qr, preferred_element_type=F32)
                dv = tv if dv is None else dv + tv
                dk = tk if dk is None else dk + tk
                dqt[rr, r] += jnp.dot(kt, ds, preferred_element_type=F32)
            acc[t, 0] += dk
            acc[t, 1] += dv

            @pl.when(t == steps - 1)
            def _():
                for r in range(R):
                    dq_send[rr, :, r * D : (r + 1) * D] = (dqt[rr, r] * scale).T.astype(BF16)

            @pl.when(jnp.logical_and(t == steps - 1, i == 0))
            def _():
                dq_copy.start()

            return carry

        lax.fori_loop(0, 2, inner, 0)

        @pl.when(d > 0)
        def _():
            part_send[d, hf] = acc[t].astype(BF16)
            part_copy(d, hf).start()

        return carry

    lax.fori_loop(0, steps, step, 0)

    def last_copy(a, b):
        c2, h2 = near_at(a, b)
        return pltpu.make_async_remote_copy(
            src_ref=last_send.at[a, :, pl.ds(pl.multiple_of(h2 * piece, piece), piece), :],
            dst_ref=last_recv.at[2 * head + core],
            send_sem=last_send_sem.at[a * n_head + b],
            recv_sem=last_recv_sem.at[a * n_head + b],
            device_id=(chip * 2 + c2, h2),
            device_id_type=MESH,
        )

    for hf in range(2):
        own = steps - 1 if hf == 0 else 0

        def add(d, total):
            part_copy(d, hf).wait_recv()
            return total + part_recv[d, hf].astype(F32)

        total = acc[own]
        for d in range(1, chips):
            total = add(d, total)
        last_send[hf, 0] = (total[0] * scale).astype(BF16)
        last_send[hf, 1] = total[1].astype(BF16)
        for a, b in near:
            if a == hf:
                last_copy(a, b).start()
    last_recv[2 * head + core] = last_send[0, :, own_rows, :]
    dq_out[:, lanes(core * R * D, R * D)] = dq_send[0]
    dq_copy.wait_recv()
    dq_out[:, lanes(mate * R * D, R * D)] = dq_recv[...]
    for a, b in near:
        last_copy(a, b).wait_recv()
    for g in range(2 * n_head):
        dk_out[:, g * D : (g + 1) * D] = last_recv[g, 0]
        dv_out[:, g * D : (g + 1) * D] = last_recv[g, 1]

    for key in sorted(first):
        first[key].wait_send()
    for copy in pair:
        copy.wait_send()
    for d in range(1, chips):
        for hf in range(2):
            kv_copy(d, hf).wait_send()
            part_copy(d, hf).wait_send()
    dq_copy.wait_send()
    for a, b in near:
        last_copy(a, b).wait_send()


def local(n_seq, n_head, queries, keys, values, outputs, out_grad, log_norm, block_order):
    D = HEAD_SIZE
    R = QUERY_HEADS // KEY_VALUE_HEADS
    chips = n_seq // 2
    rows, width = queries.shape
    piece = keys.shape[0]
    heads = log_norm.shape[0]
    anywhere = pl.BlockSpec(memory_space=pl.ANY)
    vmem = pl.BlockSpec(memory_space=pltpu.VMEM)
    dma = pltpu.SemaphoreType.DMA
    return pl.pallas_call(
        functools.partial(kernel, n_seq, n_head),
        out_shape=(
            jax.ShapeDtypeStruct(queries.shape, BF16),
            jax.ShapeDtypeStruct(keys.shape, BF16),
            jax.ShapeDtypeStruct(values.shape, BF16),
        ),
        in_specs=[anywhere] * 6 + [pl.BlockSpec(memory_space=pltpu.SMEM)],
        out_specs=(vmem, vmem, vmem),
        scratch_shapes=[
            pltpu.VMEM((2, R, rows, D), BF16),
            pltpu.VMEM((2, R, rows, D), BF16),
            pltpu.VMEM((rows, width), BF16),
            pltpu.VMEM((rows, width), BF16),
            pltpu.VMEM((2, heads, rows), F32),
            pltpu.VMEM((2, heads, rows), F32),
            pltpu.VMEM((chips, 2, 2, rows, D), BF16),
            pltpu.VMEM((2 * chips, 2, rows, D), F32),
            pltpu.VMEM((2, R, D, rows), F32),
            pltpu.VMEM((2, rows, R * D), BF16),
            pltpu.VMEM((rows, R * D), BF16),
            pltpu.VMEM((chips, 2, 2, rows, D), BF16),
            pltpu.VMEM((chips, 2, 2, rows, D), BF16),
            pltpu.VMEM((2, 2, rows, D), BF16),
            pltpu.VMEM((2 * n_head, 2, piece, D), BF16),
            dma((5 + 2 * R,)),
            dma((2 * n_head, 2)),
            dma((2 * n_head, 2)),
            dma((2 * R + 2,)),
            dma((2 * R + 2,)),
            dma((chips, 2)),
            dma((chips, 2)),
            dma((chips, 2)),
            dma((chips, 2)),
            dma((2 * n_head,)),
            dma((2 * n_head,)),
            dma((2,)),
        ],
        compiler_params=pltpu.CompilerParams(
            collective_id=0, has_side_effects=True, vmem_limit_bytes=56 * 1024 * 1024
        ),
    )(queries, keys, values, outputs, out_grad, log_norm, block_order)


def solution(mesh):
    in_specs = (
        P("seq", "head"),
        P(("seq", "head"), None),
        P(("seq", "head"), None),
        P("seq", "head"),
        P("seq", "head"),
        P("head", "seq"),
        P(),
    )
    out_specs = (P("seq", "head"), P(("seq", "head"), None), P(("seq", "head"), None))
    body = functools.partial(local, mesh.shape["seq"], mesh.shape["head"])
    return jax.shard_map(body, mesh=mesh, in_specs=in_specs, out_specs=out_specs, check_vma=False)
```

time: 189 us -> 47 us (0.25)
  waiting for transfers between devices: 79.9 us -> 0 us
  Pallas kernels: 0 us -> 42 us
  local copies, waits for them, and re-layouts: 31.1 us -> 3.51 us
  blocking collectives: 20.6 us -> 0 us
  matrix products: 19.5 us -> 0 us
  starting transfers between devices: 19.4 us -> 0 us
  between operations: 15.1 us -> 0.65 us
    pallas_call x0 -> x1, Pallas kernels: none -> 42 us  [local(): pl.pallas_call(functools.partial(kernel, n_seq, n_head), out_shape=(jax.S...]
    all_gather x2 -> x0, waiting for transfers between devices: 33.4 us -> none  [the longest x1 33.3 us: local(): dout_piece = lax.all_gather(out_grad, 'seq', axis=0, tiled=True)]
    reduce_scatter x1 -> x0, waiting for transfers between devices: 29.6 us -> none  [local(): lax.psum_scatter(grad_q_all.astype(jnp.bfloat16), 'seq', scatter_dimensio...]
    all_gather x2 -> x0, blocking collectives: 20.6 us -> none  [the longest x1 12.3 us: local(): lax.all_gather(delta, 'seq', axis=0, tiled=True)]
    dot_general x10 -> x0, matrix products: 19.5 us -> none  [the longest x2 8.49 us: masked_terms(): jnp.einsum('tgrd,ngd->grtn', dout_blk, v_blk, preferred_element_type=jnp....]
    all_to_all x4 -> x0, starting transfers between devices: 19.3 us -> none  [the longest x1 6.35 us: local(): lax.all_to_all(keys, 'head', split_axis=1, concat_axis=0, tiled=True)]
    all_to_all x4 -> x0, waiting for transfers between devices: 16.9 us -> none  [the longest x1 6.25 us: local(): lax.all_to_all(values, 'head', split_axis=1, concat_axis=0, tiled=True)]
    convert_element_type x5 -> x0, local copies, waits for them, and re-layouts: 7.92 us -> none  [the longest x1 6.2 us: local(): grad_q_all.astype(jnp.bfloat16)]
  transfers between devices with their start and end apart: 7 -> 0, of which waited for: 5 -> 0; matrix products, arithmetic and copies ran while one was open for 6% -> 0% of each run, Pallas kernels for 0% -> 0%
where the time goes in v1:
time: 47 us; the launch traced here: 46.1 us
  Pallas kernels  42 us (89%)
  local copies, waits for them, and re-layouts  3.51 us (7%)
  between operations  0.65 us (1%)
    pallas_call x1, Pallas kernels, local(): pl.pallas_call(functools.partial(kernel, n_seq, n_head), out_shape=(jax.S...  42 us
    unnamed x7, local copies, waits for them, and re-layouts  3.51 us

profile of v1, /device:TPU:0, one launch (start us, length us, event | category | flops | bytes accessed | tf_op | source)
XLA Modules:
  0.0 46.1 jit_solution(14216332331236066935)
XLA Ops:
  0.6 42.0 %shard_map.94 = (bf16[256,1024]{1,0:T(8,128)(2,1)}, bf16[64,1024]{1,0:T(8,128)(2,1)}, bf16[64,1024]{1,0:T(8,128)(2,1)}) custom-call(bf16[256,1024]{1,0:T(8,128)(2,1)} %q_in.1, bf16[64,1024]{1,0:T(8,128)(2,1)} %k_in.1, bf16[64,1024]{1,0:T(8,128)(2,1)} %v_in.1, bf16[256,1024]{1,0:T(8,128)(2,1)} %o_in.1, bf16[256,1024]{1,0:T(8,128)(2,1)} %do_in.1, ...), custom_call_target="tpu_custom_call" | custom-call | tf_op jit(solution)/shard_map/pallas_call | solution.py:325
  42.6 0.0 copy-start.1
  42.6 1.9 %copy.13 = bf16[256,1024]{1,0:T(8,128)(2,1)} copy(bf16[256,1024]{1,0:T(8,128)(2,1)} %get-tuple-element.6) | data formatting | bytes 1048576
  44.5 0.0 copy-done.1
  44.5 0.0 copy-start
  44.5 0.7 %copy.14 = bf16[64,1024]{1,0:T(8,128)(2,1)} copy(bf16[64,1024]{1,0:T(8,128)(2,1)S(1)} %copy-done.1) | data formatting | bytes 262144
  45.2 0.3 copy-done
  45.5 0.7 %copy.15 = bf16[64,1024]{1,0:T(8,128)(2,1)} copy(bf16[64,1024]{1,0:T(8,128)(2,1)S(1)} %copy-done) | data formatting | bytes 262144
Async XLA Ops:
  42.6 1.9 %copy-start.1 = (bf16[64,1024]{1,0:T(8,128)(2,1)S(1)}, bf16[64,1024]{1,0:T(8,128)(2,1)}, u32[]{:S(2)}) copy-start(bf16[64,1024]{1,0:T(8,128)(2,1)} %get-tuple-element.7) | copy-start | bytes 393220
  44.5 1.0 %copy-start = (bf16[64,1024]{1,0:T(8,128)(2,1)S(1)}, bf16[64,1024]{1,0:T(8,128)(2,1)}, u32[]{:S(2)}) copy-start(bf16[64,1024]{1,0:T(8,128)(2,1)} %get-tuple-element.8) | copy-start | bytes 393220

commit v2 on v1

v2 whole, which is shorter than its diff:
```python
import functools
import math

import jax
import jax.numpy as jnp
from jax import lax
from jax.experimental import pallas as pl
from jax.experimental.pallas import tpu as pltpu
from jax.sharding import PartitionSpec as P

QUERY_HEADS = 32
KEY_VALUE_HEADS = 8
HEAD_SIZE = 128
MESH = pl.DeviceIdType.MESH
NT = (((1,), (1,)), ((), ()))
F32 = jnp.float32
BF16 = jnp.bfloat16
AHEAD = 3
LAG = 2


def kernel(
    n_seq,
    n_head,
    q_in,
    k_in,
    v_in,
    o_in,
    do_in,
    lse_in,
    order,
    dq_out,
    dk_out,
    dv_out,
    qs,
    dos,
    o_all,
    do_all,
    lse,
    delta,
    kv,
    acc,
    own_acc,
    dqt,
    dq_send,
    dq_recv,
    part_send,
    part_recv,
    last_send,
    last_recv,
    load_sem,
    first_send_sem,
    first_recv_sem,
    pair_send_sem,
    pair_recv_sem,
    kv_send_sem,
    kv_recv_sem,
    part_send_sem,
    part_recv_sem,
    last_send_sem,
    last_recv_sem,
    dq_sem,
):
    D = HEAD_SIZE
    R = QUERY_HEADS // KEY_VALUE_HEADS
    chips = n_seq // 2
    bits = (chips - 1).bit_length()
    steps = 2 * chips
    rows = q_in.shape[0]
    half = rows // 2
    piece = k_in.shape[0]
    me_s = lax.axis_index("seq")
    head = lax.axis_index("head")
    core = me_s % 2
    chip = me_s // 2
    mate = (core + 1) % 2
    mate_id = (chip * 2 + mate, head)
    scale = D ** (-0.5)

    def flip(a, d):
        return sum(((a // 2**i) % 2 + (d // 2**i) % 2) % 2 * 2**i for i in range(bits))

    def peer(d):
        return (flip(chip, d) * 2 + core, head)

    last = 2 * n_head - 1
    seg = min(chips, 4)
    chunks = chips // seg
    keys_here = seg * piece

    def block(t):
        m = (t + last) % (last + 1)
        end = t // last
        mid = ((t + last - 1) // last) * (1 - end)
        near_b = m // 4 + 1
        b = near_b + ((m // 2) % 2) * (n_head - 2 * near_b)
        return mid * (m % 2) + end, mid * b

    near = []
    for b in range(1, n_head // 2 + 1):
        for bb in sorted({b, n_head - b}):
            near += [(0, bb), (1, bb)]
    near.append((1, 0))

    def to_at(a, b):
        return (chip * 2 + (core + a) % 2, (head + b) % n_head)

    def from_at(a, b):
        return (chip * 2 + (core + a) % 2, (head + n_head - b) % n_head)

    def lanes(start, size):
        return pl.ds(pl.multiple_of(start, D), size)

    mine = lanes((2 * head + core) * D, D)
    kv_loads = [
        pltpu.make_async_copy(k_in.at[:, mine], kv.at[0, 0, 0, 0], load_sem.at[3]),
        pltpu.make_async_copy(v_in.at[:, mine], kv.at[0, 0, 1, 0], load_sem.at[4]),
    ]
    loads = [
        pltpu.make_async_copy(o_in, o_all, load_sem.at[0]),
        pltpu.make_async_copy(do_in, do_all, load_sem.at[1]),
        pltpu.make_async_copy(lse_in, lse.at[0], load_sem.at[2]),
    ]
    for r in range(R):
        cols = lanes((core * R + r) * D, D)
        loads.append(pltpu.make_async_copy(q_in.at[:, cols], qs.at[0, r], load_sem.at[5 + r]))
        loads.append(pltpu.make_async_copy(do_in.at[:, cols], dos.at[0, r], load_sem.at[5 + R + r]))
    for copy in kv_loads + loads:
        copy.start()

    barrier = pltpu.get_barrier_semaphore()
    for a, b in near:
        pl.semaphore_signal(barrier, inc=1, device_id=to_at(a, b), device_id_type=MESH)
    for d in range(1, chips):
        pl.semaphore_signal(barrier, inc=1, device_id=peer(d), device_id_type=MESH)
    pl.semaphore_wait(barrier, len(near) + chips - 1)

    def near_copy(a, b, j):
        target = to_at(a, b)
        src = (k_in, v_in)[j]
        return pltpu.make_async_remote_copy(
            src_ref=src.at[:, lanes((2 * target[1] + target[0] % 2) * D, D)],
            dst_ref=kv.at[a, b, j, 0],
            send_sem=first_send_sem.at[a * n_head + b, j],
            recv_sem=first_recv_sem.at[a * n_head + b, j],
            device_id=target,
            device_id_type=MESH,
        )

    def kv_copy(a, b, d):
        return pltpu.make_async_remote_copy(
            src_ref=kv.at[a, b, :, 0],
            dst_ref=kv.at[a, b, :, d],
            send_sem=kv_send_sem.at[a * n_head + b, d],
            recv_sem=kv_recv_sem.at[a * n_head + b, d],
            device_id=peer(d),
            device_id_type=MESH,
        )

    def part_copy(a, b, d):
        return pltpu.make_async_remote_copy(
            src_ref=part_send.at[a, b, d],
            dst_ref=part_recv.at[a, b, d],
            send_sem=part_send_sem.at[a * n_head + b, d],
            recv_sem=part_recv_sem.at[a * n_head + b, d],
            device_id=peer(d),
            device_id_type=MESH,
        )

    def last_copy(a, b):
        return pltpu.make_async_remote_copy(
            src_ref=last_send.at[a, b],
            dst_ref=last_recv.at[2 * head + core],
            send_sem=last_send_sem.at[a * n_head + b],
            recv_sem=last_recv_sem.at[a * n_head + b],
            device_id=from_at(a, b),
            device_id_type=MESH,
        )

    def to_mate(src, dst, i):
        return pltpu.make_async_remote_copy(
            src_ref=src,
            dst_ref=dst,
            send_sem=pair_send_sem.at[i],
            recv_sem=pair_recv_sem.at[i],
            device_id=mate_id,
            device_id_type=MESH,
        )

    def forward(t):
        a, b = block(t)
        near_copy(a, b, 0).wait_recv()
        near_copy(a, b, 1).wait_recv()
        for d in range(1, chips):
            kv_copy(a, b, d).start()

    for copy in kv_loads:
        copy.wait()
    for d in range(1, chips):
        kv_copy(0, 0, d).start()
    for a, b in near:
        near_copy(a, b, 0).start()
        near_copy(a, b, 1).start()
    pair = []
    for r in range(R):
        cols = lanes((mate * R + r) * D, D)
        pair.append(to_mate(q_in.at[:, cols], qs.at[1, r], r))
        pair.append(to_mate(do_in.at[:, cols], dos.at[1, r], R + r))
    pair.append(to_mate(lse_in, lse.at[1], 2 * R))
    for copy in pair:
        copy.start()

    for copy in loads:
        copy.wait()
    for i in range(2 * R):
        prod = o_all[:, i * D : (i + 1) * D].astype(F32) * do_all[:, i * D : (i + 1) * D].astype(F32)
        delta[0, pl.ds(i, 1), :] = jnp.sum(prod.T, axis=0, keepdims=True)
    dqt[...] = jnp.zeros_like(dqt)
    send_delta = to_mate(delta.at[0], delta.at[1], 2 * R + 1)
    forward(1)
    send_delta.start()
    pair.append(send_delta)
    for t in range(2, AHEAD):
        forward(t)
    for copy in pair:
        copy.wait_recv()

    dq_copy = pltpu.make_async_remote_copy(
        src_ref=dq_send.at[1],
        dst_ref=dq_recv,
        send_sem=dq_sem.at[0],
        recv_sem=dq_sem.at[1],
        device_id=mate_id,
        device_id_type=MESH,
    )

    def reduce(t):
        a, b = block(t)
        total = own_acc[a, b]
        for d in range(1, chips):
            part_copy(a, b, d).wait_recv()
            total = total + part_recv[a, b, d].astype(F32)
        last_send[a, b, 0] = (total[0] * scale).astype(BF16)
        last_send[a, b, 1] = total[1].astype(BF16)

    def spots(index):
        off = lax.broadcasted_iota(jnp.int32, (1, rows), 1)
        b0 = order[2 * index]
        b1 = order[2 * index + 1]
        return off + jnp.where(off < half, b0 * half, b1 * half - half)

    def step(t, carry):
        a, b = block(t)
        from_core = (core + a) % 2
        from_row = ((head + n_head - b) % n_head) * piece

        @pl.when(t + AHEAD <= last)
        def _():
            forward(t + AHEAD)

        def chunk(c, carry):
            d0 = c * seg
            for e in range(seg):
                if e > 0:
                    kv_copy(a, b, d0 + e).wait_recv()
                elif chunks > 1:

                    @pl.when(c > 0)
                    def _():
                        kv_copy(a, b, d0).wait_recv()

            def inner(i, carry):
                rr = (i + t // last) % 2
                kk = kv[a, b, 0, pl.ds(d0, seg)].reshape(keys_here, D)
                vv = kv[a, b, 1, pl.ds(d0, seg)].reshape(keys_here, D)
                kt = kk.T
                off = lax.broadcasted_iota(jnp.int32, (keys_here, 1), 0)
                k_at = off
                for e in range(seg):
                    index = flip(chip, d0 + e) * 2 + from_core
                    base = order[2 * index + from_row // half] * half + from_row % half - e * piece
                    k_at = jnp.where(off >= e * piece, off + base, k_at)
                q_at = spots(chip * 2 + (core + rr) % 2)
                mask = k_at <= q_at
                dk = None
                dv = None
                for r in range(R):
                    qr = qs[rr, r]
                    dor = dos[rr, r]
                    s = lax.dot_general(kk, qr, NT, preferred_element_type=F32)
                    dp = lax.dot_general(vv, dor, NT, preferred_element_type=F32)
                    row = pl.ds(core * R + r, 1)
                    l2 = lse[rr, row, :] * math.log2(math.e)
                    dl = delta[rr, row, :]
                    prob = jnp.where(mask, jnp.exp2(s * (scale * math.log2(math.e)) - l2), 0.0)
                    ds = (prob * (dp - dl)).astype(BF16)
                    tv = jnp.dot(prob.astype(BF16), dor, preferred_element_type=F32)
                    tk = jnp.dot(ds, qr, preferred_element_type=F32)
                    dv = tv if dv is None else dv + tv
                    dk = tk if dk is None else dk + tk
                    dqt[rr, r] += jnp.dot(kt, ds, preferred_element_type=F32)

                @pl.when(i == 0)
                def _():
                    acc[0] = dk
                    acc[1] = dv

                @pl.when(i == 1)
                def _():
                    acc[0] += dk
                    acc[1] += dv

                @pl.when(jnp.logical_and(t == last, c == chunks - 1))
                def _():
                    for r in range(R):
                        dq_send[rr, :, r * D : (r + 1) * D] = (dqt[rr, r] * scale).T.astype(BF16)

                @pl.when(jnp.logical_and(jnp.logical_and(t == last, c == chunks - 1), i == 0))
                def _():
                    dq_copy.start()

                return carry

            lax.fori_loop(0, 2, inner, 0)
            for e in range(seg):
                here = slice(e * piece, (e + 1) * piece)
                if e > 0:
                    part_send[a, b, d0 + e] = acc[:, here, :].astype(BF16)
                    part_copy(a, b, d0 + e).start()
                elif chunks > 1:

                    @pl.when(c == 0)
                    def _():
                        own_acc[a, b] = acc[:, here, :]

                    @pl.when(c > 0)
                    def _():
                        part_send[a, b, d0] = acc[:, here, :].astype(BF16)
                        part_copy(a, b, d0).start()

                else:
                    own_acc[a, b] = acc[:, here, :]
            return carry

        if chunks > 1:
            lax.fori_loop(0, chunks, chunk, 0)
        else:
            chunk(0, 0)

        @pl.when(t == LAG)
        def _():
            reduce(0)

        @pl.when(t > LAG)
        def _():
            reduce(t - LAG)
            last_copy(*block(t - LAG)).start()

        return carry

    lax.fori_loop(0, last + 1, step, 0)
    for t in range(last + 1 - LAG, last + 1):
        reduce(t)
        last_copy(*block(t)).start()
    last_recv[2 * head + core] = last_send[0, 0]
    dq_out[:, lanes(core * R * D, R * D)] = dq_send[0]
    dq_copy.wait_recv()
    dq_out[:, lanes(mate * R * D, R * D)] = dq_recv[...]
    for a, b in near:
        last_copy(a, b).wait_recv()
    for g in range(2 * n_head):
        dk_out[:, g * D : (g + 1) * D] = last_recv[g, 0]
        dv_out[:, g * D : (g + 1) * D] = last_recv[g, 1]

    for copy in pair:
        copy.wait_send()
    dq_copy.wait_send()
    for a, b in near:
        near_copy(a, b, 0).wait_send()
        near_copy(a, b, 1).wait_send()
        last_copy(a, b).wait_send()
    for a, b in [(0, 0)] + near:
        for d in range(1, chips):
            kv_copy(a, b, d).wait_send()
            part_copy(a, b, d).wait_send()


def local(n_seq, n_head, queries, keys, values, outputs, out_grad, log_norm, block_order):
    D = HEAD_SIZE
    R = QUERY_HEADS // KEY_VALUE_HEADS
    chips = n_seq // 2
    rows, width = queries.shape
    piece = keys.shape[0]
    heads = log_norm.shape[0]
    anywhere = pl.BlockSpec(memory_space=pl.ANY)
    vmem = pl.BlockSpec(memory_space=pltpu.VMEM)
    dma = pltpu.SemaphoreType.DMA
    return pl.pallas_call(
        functools.partial(kernel, n_seq, n_head),
        out_shape=(
            jax.ShapeDtypeStruct(queries.shape, BF16),
            jax.ShapeDtypeStruct(keys.shape, BF16),
            jax.ShapeDtypeStruct(values.shape, BF16),
        ),
        in_specs=[anywhere] * 6 + [pl.BlockSpec(memory_space=pltpu.SMEM)],
        out_specs=(vmem, vmem, vmem),
        scratch_shapes=[
            pltpu.VMEM((2, R, rows, D), BF16),
            pltpu.VMEM((2, R, rows, D), BF16),
            pltpu.VMEM((rows, width), BF16),
            pltpu.VMEM((rows, width), BF16),
            pltpu.VMEM((2, heads, rows), F32),
            pltpu.VMEM((2, heads, rows), F32),
            pltpu.VMEM((2, n_head, 2, chips, piece, D), BF16),
            pltpu.VMEM((2, min(chips, 4) * piece, D), F32),
            pltpu.VMEM((2, n_head, 2, piece, D), F32),
            pltpu.VMEM((2, R, D, rows), F32),
            pltpu.VMEM((2, rows, R * D), BF16),
            pltpu.VMEM((rows, R * D), BF16),
            pltpu.VMEM((2, n_head, chips, 2, piece, D), BF16),
            pltpu.VMEM((2, n_head, chips, 2, piece, D), BF16),
            pltpu.VMEM((2, n_head, 2, piece, D), BF16),
            pltpu.VMEM((2 * n_head, 2, piece, D), BF16),
            dma((5 + 2 * R,)),
            dma((2 * n_head, 2)),
            dma((2 * n_head, 2)),
            dma((2 * R + 2,)),
            dma((2 * R + 2,)),
            dma((2 * n_head, chips)),
            dma((2 * n_head, chips)),
            dma((2 * n_head, chips)),
            dma((2 * n_head, chips)),
            dma((2 * n_head,)),
            dma((2 * n_head,)),
            dma((2,)),
        ],
        compiler_params=pltpu.CompilerParams(
            collective_id=0, has_side_effects=True, vmem_limit_bytes=56 * 1024 * 1024
        ),
    )(queries, keys, values, outputs, out_grad, log_norm, block_order)


def solution(mesh):
    in_specs = (
        P("seq", "head"),
        P(("seq", "head"), None),
        P(("seq", "head"), None),
        P("seq", "head"),
        P("seq", "head"),
        P("head", "seq"),
        P(),
    )
    out_specs = (P("seq", "head"), P(("seq", "head"), None), P(("seq", "head"), None))
    body = functools.partial(local, mesh.shape["seq"], mesh.shape["head"])
    return jax.shard_map(body, mesh=mesh, in_specs=in_specs, out_specs=out_specs, check_vma=False)
```

time: 47 us -> 45 us (0.957); the launches traced: 46.1 us -> 44.8 us
  Pallas kernels: 42 us -> 40.6 us
    pallas_call x1, Pallas kernels: 42 us -> 40.6 us  [local(): pl.pallas_call(functools.partial(kernel, n_seq, n_head), out_shape=(jax.S...]
where the time goes in v2:
time: 45 us; the launch traced here: 44.8 us
  Pallas kernels  40.6 us (90%)
  local copies, waits for them, and re-layouts  3.51 us (8%)
  between operations  0.65 us (1%)
    pallas_call x1, Pallas kernels, local(): pl.pallas_call(functools.partial(kernel, n_seq, n_head), out_shape=(jax.S...  40.6 us
    unnamed x7, local copies, waits for them, and re-layouts  3.51 us

profile of v2, /device:TPU:0, one launch (start us, length us, event | category | flops | bytes accessed | tf_op | source)
XLA Modules:
  0.0 44.8 jit_solution(8255235375362347098)
XLA Ops:
  0.6 40.6 %shard_map.94 = (bf16[256,1024]{1,0:T(8,128)(2,1)}, bf16[64,1024]{1,0:T(8,128)(2,1)}, bf16[64,1024]{1,0:T(8,128)(2,1)}) custom-call(bf16[256,1024]{1,0:T(8,128)(2,1)} %q_in.1, bf16[64,1024]{1,0:T(8,128)(2,1)} %k_in.1, bf16[64,1024]{1,0:T(8,128)(2,1)} %v_in.1, bf16[256,1024]{1,0:T(8,128)(2,1)} %o_in.1, bf16[256,1024]{1,0:T(8,128)(2,1)} %do_in.1, ...), custom_call_target="tpu_custom_call" | custom-call | tf_op jit(solution)/shard_map/pallas_call | solution.py:398
  41.3 0.0 copy-start.1
  41.3 1.9 %copy.13 = bf16[256,1024]{1,0:T(8,128)(2,1)} copy(bf16[256,1024]{1,0:T(8,128)(2,1)} %get-tuple-element.6) | data formatting | bytes 1048576
  43.2 0.0 copy-done.1
  43.2 0.0 copy-start
  43.2 0.7 %copy.14 = bf16[64,1024]{1,0:T(8,128)(2,1)} copy(bf16[64,1024]{1,0:T(8,128)(2,1)S(1)} %copy-done.1) | data formatting | bytes 262144
  43.9 0.3 copy-done
  44.1 0.7 %copy.15 = bf16[64,1024]{1,0:T(8,128)(2,1)} copy(bf16[64,1024]{1,0:T(8,128)(2,1)S(1)} %copy-done) | data formatting | bytes 262144
Async XLA Ops:
  41.3 1.9 %copy-start.1 = (bf16[64,1024]{1,0:T(8,128)(2,1)S(1)}, bf16[64,1024]{1,0:T(8,128)(2,1)}, u32[]{:S(2)}) copy-start(bf16[64,1024]{1,0:T(8,128)(2,1)} %get-tuple-element.7) | copy-start | bytes 393220
  43.2 1.0 %copy-start = (bf16[64,1024]{1,0:T(8,128)(2,1)S(1)}, bf16[64,1024]{1,0:T(8,128)(2,1)}, u32[]{:S(2)}) copy-start(bf16[64,1024]{1,0:T(8,128)(2,1)} %get-tuple-element.8) | copy-start | bytes 393220
